TPU v7x, 512 devices: a whole 4x4x16 slice. The times are simulated.
512 devices in a mesh: crop: 8 (over z_lo, core), axial: 64 (over x, y, z_hi).
Axes of the slice: x: 4, y: 4, z: 16 (z_hi: 4, z_lo: 4; z = z_hi * 4 + z_lo), core: 2. Of those that a mesh axis runs over, the one named last changes fastest.
Arguments:
- pair: bfloat16 [8, 256, 256, 128], P('crop', 'axial'), may hold values from -6 to 6
- crop_mask: int32 [8, 256], P('crop'), may hold values 0 or 1
- weights: bfloat16 [128, 768], replicated, may hold values from -0.5 to 0.5
- probe_signs: int32 [128, 768], replicated, may hold values from 0 to 1
Outputs:
- pair_out: bfloat16 [8, 256, 256, 128], P('crop', 'axial')
- curvature: float32 [128, 768], replicated
All inputs are finite; a program needn't handle non-finite values. No bound on the sum of `crop_mask` on one device may be relied on, other than what follows from the above.
Results may differ from a plain program's by a relative error of at most 0.006.
Values may be sent and summed in bfloat16 or wider, within the bound.
A program may use at most 64 MiB of HBM per device.

v0:
```python
import jax
import jax.numpy as jnp
from jax import lax
from jax.sharding import PartitionSpec as P


def norm_axis(value, axis):
    mean = jnp.mean(value, axis=axis, keepdims=True)
    centered = value - mean
    var = jnp.mean(centered * centered, axis=axis, keepdims=True)
    return centered * lax.rsqrt(var + 1e-05)


def project_in(w_in, zn_bf, mask_pair):
    proj = jnp.einsum(
        "rnc,cd->drn", zn_bf, w_in.astype(jnp.bfloat16), preferred_element_type=jnp.float32
    )
    hid = proj.shape[0] // 4
    a_full = jax.nn.sigmoid(proj[hid : 2 * hid]) * proj[:hid] * mask_pair
    b_full = jax.nn.sigmoid(proj[3 * hid :]) * proj[2 * hid : 3 * hid] * mask_pair
    return (a_full, b_full)


def head(w_head, x_full, zn_bf):
    chans = zn_bf.shape[2]
    w_gate = w_head[:, :chans].astype(jnp.bfloat16)
    w_out = w_head[:, chans:].astype(jnp.bfloat16)
    x_norm = norm_axis(x_full, 0).astype(jnp.bfloat16)
    out_proj = jnp.einsum("hrn,hc->rnc", x_norm, w_out, preferred_element_type=jnp.float32)
    gating = jax.nn.sigmoid(
        jnp.einsum("rnc,cd->rnd", zn_bf, w_gate, preferred_element_type=jnp.float32)
    )
    return gating * out_proj


def tri_out(left, right):
    return jnp.einsum("cik,cjk->cij", left, right, preferred_element_type=jnp.float32)


def slab_products(slabs):
    a_ch, b_ch, ta_ch, tb_ch = slabs
    x_ch = tri_out(a_ch, b_ch).astype(jnp.bfloat16)
    tx_ch = (tri_out(ta_ch, b_ch) + tri_out(a_ch, tb_ch)).astype(jnp.bfloat16)
    return (x_ch, tx_ch, a_ch, b_ch)


def shards(pair, crop_mask, weights, probe_signs):
    pair_rows = pair[0]
    rows = pair_rows.shape[0]
    width = pair_rows.shape[1]
    chans = weights.shape[0]
    h4 = weights.shape[1] - 2 * chans
    mask = crop_mask[0].astype(jnp.float32)
    start = lax.axis_index("axial") * rows
    mask_rows = lax.dynamic_slice_in_dim(mask, start, rows, 0)
    mask_pair = mask_rows[:, None] * mask[None, :]
    zn = norm_axis(pair_rows.astype(jnp.float32), 2).astype(jnp.bfloat16)
    w_all = weights.astype(jnp.float32)
    probe = (2 * probe_signs - 1).astype(jnp.float32) * (1.0 / jnp.sqrt(jnp.float32(chans)))
    w_in, w_head = (w_all[:, :h4], w_all[:, h4:])
    v_in, v_head = (probe[:, :h4], probe[:, h4:])
    fin = lambda w: project_in(w, zn, mask_pair)
    (a_f, b_f), pull_in = jax.vjp(fin, w_in)
    _, (ta_f, tb_f) = jax.jvp(fin, (w_in,), (v_in,))
    a_bf, b_bf = (a_f.astype(jnp.bfloat16), b_f.astype(jnp.bfloat16))
    ta_bf, tb_bf = (ta_f.astype(jnp.bfloat16), tb_f.astype(jnp.bfloat16))
    a_ch, b_ch = (
        lax.all_to_all(a_bf, "axial", split_axis=0, concat_axis=1, tiled=True),
        lax.all_to_all(b_bf, "axial", split_axis=0, concat_axis=1, tiled=True),
    )
    ta_ch, tb_ch = (
        lax.all_to_all(ta_bf, "axial", split_axis=0, concat_axis=1, tiled=True),
        lax.all_to_all(tb_bf, "axial", split_axis=0, concat_axis=1, tiled=True),
    )
    x_ch, tx_ch, a_ch, b_ch = slab_products((a_ch, b_ch, ta_ch, tb_ch))
    x_bf, tx_bf = (
        lax.all_to_all(x_ch, "axial", split_axis=1, concat_axis=0, tiled=True),
        lax.all_to_all(tx_ch, "axial", split_axis=1, concat_axis=0, tiled=True),
    )
    fhead = lambda w, xx: head(w, xx, zn)
    out, pull_head = jax.vjp(fhead, w_head, x_bf.astype(jnp.float32))
    _, t_out = jax.jvp(
        fhead, (w_head, x_bf.astype(jnp.float32)), (v_head, tx_bf.astype(jnp.float32))
    )
    total = lax.axis_size("crop") * width * width
    cot = t_out * (1.0 / total)
    g_head, x_bar = pull_head(cot)
    g_head_sum = lax.psum(g_head, ("crop", "axial"))
    xb_ch = lax.all_to_all(
        x_bar.astype(jnp.bfloat16), "axial", split_axis=0, concat_axis=1, tiled=True
    )
    a_bar = jnp.einsum("cij,cjk->cik", xb_ch, b_ch, preferred_element_type=jnp.float32).astype(
        jnp.bfloat16
    )
    b_bar = jnp.einsum("cij,cik->cjk", xb_ch, a_ch, preferred_element_type=jnp.float32).astype(
        jnp.bfloat16
    )
    a_back, b_back = (
        lax.all_to_all(a_bar, "axial", split_axis=1, concat_axis=0, tiled=True),
        lax.all_to_all(b_bar, "axial", split_axis=1, concat_axis=0, tiled=True),
    )
    g_in = pull_in((a_back.astype(jnp.float32), b_back.astype(jnp.float32)))[0]
    g_in_sum = lax.psum(g_in, ("crop", "axial"))
    curvature = jnp.concatenate([g_in_sum, g_head_sum], axis=1)
    new_pair = (pair_rows.astype(jnp.float32) + out).astype(jnp.bfloat16)
    return (new_pair[None], curvature)


def solution(mesh):
    placed = (P("crop", "axial", None, None), P("crop", None), P(), P())
    return jax.shard_map(
        shards,
        mesh=mesh,
        in_specs=placed,
        out_specs=(P("crop", "axial", None, None), P()),
        check_vma=False,
    )
```

profile of v0, /device:TPU:2, one launch (start us, length us, event | category | flops | bytes accessed | tf_op | source)
XLA Modules:
  0.0 779.2 jit_solution(10818521390159609590)
XLA Ops:
  13.0 1.8 fusion.63
  15.0 2.1 fusion.38
  18.0 21.3 %all-to-all-start.4 = ((bf16[128,4,256]{2,1,0:T(4,128)(2,1)}), bf16[128,4,256]{2,1,0:T(4,128)(2,1)S(1)}, u32[]{:S(2)}, u32[]{:S(2)}) async-start(bf16[128,4,256]{2,1,0:T(4,128)(2,1)} %copy.69), calls=%async_computation.4 | async-start | bytes 524288 | tf_op jit(solution)/shard_map/all_to_all | solution.py:73
  40.1 20.7 %all-to-all-done.4 = bf16[128,4,256]{2,1,0:T(4,128)(2,1)S(1)} async-done(((bf16[128,4,256]{2,1,0:T(4,128)(2,1)}), bf16[128,4,256]{2,1,0:T(4,128)(2,1)S(1)}, u32[]{:S(2)}, u32[]{:S(2)}) %all-to-all-start.4) | async-done | bytes 262176 | tf_op jit(solution)/shard_map/all_to_all | solution.py:73
  60.9 7.8 all-to-all-start.1
  69.6 16.7 %all-to-all-done.1 = bf16[128,4,256]{2,1,0:T(4,128)(2,1)S(1)} async-done(((bf16[128,4,256]{2,1,0:T(4,128)(2,1)}), bf16[128,4,256]{2,1,0:T(4,128)(2,1)S(1)}, u32[]{:S(2)}, u32[]{:S(2)}) %all-to-all-start.1) | async-done | bytes 262176 | tf_op jit(solution)/shard_map/all_to_all | solution.py:69
  86.3 9.7 %all-to-all-start = ((bf16[128,4,256]{2,1,0:T(4,128)(2,1)}), bf16[128,4,256]{2,1,0:T(4,128)(2,1)S(1)}, u32[]{:S(2)}, u32[]{:S(2)}) async-start(bf16[128,4,256]{2,1,0:T(4,128)(2,1)} %copy.55), calls=%async_computation | async-start | bytes 524288 | tf_op jit(solution)/shard_map/all_to_all | solution.py:68
  96.8 20.0 %all-to-all-done = bf16[128,4,256]{2,1,0:T(4,128)(2,1)S(1)} async-done(((bf16[128,4,256]{2,1,0:T(4,128)(2,1)}), bf16[128,4,256]{2,1,0:T(4,128)(2,1)S(1)}, u32[]{:S(2)}, u32[]{:S(2)}) %all-to-all-start) | async-done | bytes 262176 | tf_op jit(solution)/shard_map/all_to_all | solution.py:68
  116.8 6.6 all-to-all-start.3
  126.1 18.4 %all-to-all-done.3 = bf16[128,4,256]{2,1,0:T(4,128)(2,1)} async-done(((bf16[128,4,256]{2,1,0:T(4,128)(2,1)}), bf16[128,4,256]{2,1,0:T(4,128)(2,1)}, u32[]{:S(2)}, u32[]{:S(2)}) %all-to-all-start.3) | async-done | bytes 262176 | tf_op jit(solution)/shard_map/all_to_all | solution.py:72
  144.5 6.1 all-to-all-start.2
  152.4 1.7 copy.66
  154.1 1.7 all_to_all.105
  158.3 13.6 %all-to-all-done.2 = bf16[2,256,256]{2,0,1:T(2,128)(2,1)S(1)} async-done(((bf16[2,256,256]{2,0,1:T(2,128)(2,1)}), bf16[2,256,256]{2,0,1:T(2,128)(2,1)S(1)}, u32[]{:S(2)}, u32[]{:S(2)}) %all-to-all-start.2) | async-done | bytes 262176 | tf_op jit(solution)/shard_map/all_to_all | solution.py:77
  171.9 7.0 all-to-all-start.5
  184.7 15.3 %all-to-all-done.5 = bf16[2,256,256]{2,0,1:T(2,128)(2,1)} async-done(((bf16[2,256,256]{2,0,1:T(2,128)(2,1)}), bf16[2,256,256]{2,0,1:T(2,128)(2,1)}, u32[]{:S(2)}, u32[]{:S(2)}) %all-to-all-start.5) | async-done | bytes 262176 | tf_op jit(solution)/shard_map/all_to_all | solution.py:78
  202.0 1.9 copy_bitcast_fusion
  204.0 2.2 reshape.106
  206.2 1.9 multiply_reduce_fusion
  214.2 27.7 %all_to_all.126 = bf16[128,4,256]{2,1,0:T(4,128)(2,1)S(1)} all-to-all(bf16[128,4,256]{2,1,0:T(4,128)(2,1)S(1)} %copy.75), channel_id=1, replica_groups=mesh['crop'=8,'axial'=64] {'axial'}, dimensions={0} | all-to-all | bytes 524288 | tf_op jit(solution)/shard_map/all_to_all | solution.py:89
  243.8 6.8 all-to-all-start.8
  252.9 16.5 %all-to-all-done.8 = bf16[2,256,256]{2,0,1:T(2,128)(2,1)} async-done(((bf16[2,256,256]{2,0,1:T(2,128)(2,1)}), bf16[2,256,256]{2,0,1:T(2,128)(2,1)}, u32[]{:S(2)}, u32[]{:S(2)}) %all-to-all-start.8) | async-done | bytes 262176 | tf_op jit(solution)/shard_map/all_to_all | solution.py:99
  269.4 8.6 %all-to-all-start.7 = ((bf16[2,256,256]{2,0,1:T(2,128)(2,1)}), bf16[2,256,256]{2,0,1:T(2,128)(2,1)}, u32[]{:S(2)}, u32[]{:S(2)}) async-start(bf16[2,256,256]{2,0,1:T(2,128)(2,1)} %copy.78), calls=%async_computation.7 | async-start | bytes 524288 | tf_op jit(solution)/shard_map/all_to_all | solution.py:100
  279.4 1.6 fusion.28
  281.7 1.8 copy.83
  283.5 2.0 copy.84
  285.6 12.7 %all-to-all-done.7 = bf16[2,256,256]{2,0,1:T(2,128)(2,1)} async-done(((bf16[2,256,256]{2,0,1:T(2,128)(2,1)}), bf16[2,256,256]{2,0,1:T(2,128)(2,1)}, u32[]{:S(2)}, u32[]{:S(2)}) %all-to-all-start.7) | async-done | bytes 262176 | tf_op jit(solution)/shard_map/all_to_all | solution.py:100
  298.2 1.8 copy.79
  300.1 2.1 copy.80
  302.1 1.6 multiply_multiply_fusion.3
  306.0 464.6 %all-reduce.9.cloned.1.call-done = (f32[128,256]{1,0:T(8,128)}, f32[128,512]{1,0:T(8,128)}) async-done(((f32[128,256]{1,0:T(8,128)}, f32[128,512]{1,0:T(8,128)}), (f32[128,256]{1,0:T(8,128)}, f32[128,512]{1,0:T(8,128)})) %all-reduce.9.cloned.1.call-update) | async-done | bytes 393232 | tf_op jit(solution)/shard_map/psum | solution.py:88
  770.6 1.8 pad_maximum_fusion
  (85 shorter events, 38.4 us)
Async XLA Ops:
  7.2 5.8 copy-start
  11.4 3.4 copy-start.14
  18.0 42.9 %all-to-all-start.4 = ((bf16[128,4,256]{2,1,0:T(4,128)(2,1)}), bf16[128,4,256]{2,1,0:T(4,128)(2,1)S(1)}, u32[]{:S(2)}, u32[]{:S(2)}) async-start(bf16[128,4,256]{2,1,0:T(4,128)(2,1)} %copy.69), calls=%async_computation.4 | async-start | bytes 524288 | tf_op jit(solution)/shard_map/all_to_all | solution.py:73
  60.9 25.4 %all-to-all-start.1 = ((bf16[128,4,256]{2,1,0:T(4,128)(2,1)}), bf16[128,4,256]{2,1,0:T(4,128)(2,1)S(1)}, u32[]{:S(2)}, u32[]{:S(2)}) async-start(bf16[128,4,256]{2,1,0:T(4,128)(2,1)} %copy.57), calls=%async_computation.1 | async-start | bytes 524288 | tf_op jit(solution)/shard_map/all_to_all | solution.py:69
  86.3 30.6 %all-to-all-start = ((bf16[128,4,256]{2,1,0:T(4,128)(2,1)}), bf16[128,4,256]{2,1,0:T(4,128)(2,1)S(1)}, u32[]{:S(2)}, u32[]{:S(2)}) async-start(bf16[128,4,256]{2,1,0:T(4,128)(2,1)} %copy.55), calls=%async_computation | async-start | bytes 524288 | tf_op jit(solution)/shard_map/all_to_all | solution.py:68
  116.8 6.6 copy-start.13
  116.8 27.6 %all-to-all-start.3 = ((bf16[128,4,256]{2,1,0:T(4,128)(2,1)}), bf16[128,4,256]{2,1,0:T(4,128)(2,1)}, u32[]{:S(2)}, u32[]{:S(2)}) async-start(bf16[128,4,256]{2,1,0:T(4,128)(2,1)} %copy.65), calls=%async_computation.3 | async-start | bytes 524288 | tf_op jit(solution)/shard_map/all_to_all | solution.py:72
  123.6 32.2 %copy-start.8 = (bf16[2,256,256]{2,1,0:T(8,128)(2,1)}, bf16[2,256,256]{2,1,0:T(8,128)(2,1)S(1)}, u32[]{:S(2)}) copy-start(bf16[2,256,256]{2,1,0:T(8,128)(2,1)S(1)} %all_to_all.100) | copy-start | bytes 786436
  124.8 32.2 %copy-start.6 = (bf16[2,256,256]{2,1,0:T(8,128)(2,1)}, bf16[2,256,256]{2,1,0:T(8,128)(2,1)S(1)}, u32[]{:S(2)}) copy-start(bf16[2,256,256]{2,1,0:T(8,128)(2,1)S(1)} %all_to_all.96) | copy-start | bytes 786436
  144.5 27.4 %all-to-all-start.2 = ((bf16[2,256,256]{2,0,1:T(2,128)(2,1)}), bf16[2,256,256]{2,0,1:T(2,128)(2,1)S(1)}, u32[]{:S(2)}, u32[]{:S(2)}) async-start(bf16[2,256,256]{2,0,1:T(2,128)(2,1)} %copy.59), calls=%async_computation.2 | async-start | bytes 524288 | tf_op jit(solution)/shard_map/all_to_all | solution.py:77
  171.9 8.3 %copy-start.10 = (bf16[2,256,256]{2,0,1:T(2,128)(2,1)}, bf16[2,256,256]{2,0,1:T(2,128)(2,1)S(1)}, u32[]{:S(2)}) copy-start(bf16[2,256,256]{2,0,1:T(2,128)(2,1)S(1)} %all-to-all-done.2) | copy-start | bytes 786436
  171.9 28.1 %all-to-all-start.5 = ((bf16[2,256,256]{2,0,1:T(2,128)(2,1)}), bf16[2,256,256]{2,0,1:T(2,128)(2,1)}, u32[]{:S(2)}, u32[]{:S(2)}) async-start(bf16[2,256,256]{2,0,1:T(2,128)(2,1)} %copy.71), calls=%async_computation.5 | async-start | bytes 524288 | tf_op jit(solution)/shard_map/all_to_all | solution.py:78
  183.7 0.8 copy-start.4
  201.1 0.8 copy-start.5
  206.2 3.0 copy-start.12
  208.2 2.2 copy-start.7
  209.2 3.4 copy-start.1
  212.6 1.4 copy-start.3
  213.7 28.4 %copy-start.9 = (bf16[2,256,256]{2,1,0:T(8,128)(2,1)S(1)}, bf16[2,256,256]{2,1,0:T(8,128)(2,1)}, u32[]{:S(2)}) copy-start(bf16[2,256,256]{2,1,0:T(8,128)(2,1)} %copy-done.8) | copy-start | bytes 786436
  242.1 0.7 copy-start.11
  242.8 36.6 %copy-start.2 = (f32[4,256,128]{2,1,0:T(8,128)S(1)}, f32[4,256,128]{2,1,0:T(8,128)}, u32[]{:S(2)}) copy-start(f32[4,256,128]{2,1,0:T(8,128)} %copy-done.1) | copy-start | bytes 1572868
  243.8 25.6 %all-to-all-start.8 = ((bf16[2,256,256]{2,0,1:T(2,128)(2,1)}), bf16[2,256,256]{2,0,1:T(2,128)(2,1)}, u32[]{:S(2)}, u32[]{:S(2)}) async-start(bf16[2,256,256]{2,0,1:T(2,128)(2,1)} %copy.82), calls=%async_computation.8 | async-start | bytes 524288 | tf_op jit(solution)/shard_map/all_to_all | solution.py:99
  269.4 28.8 %all-to-all-start.7 = ((bf16[2,256,256]{2,0,1:T(2,128)(2,1)}), bf16[2,256,256]{2,0,1:T(2,128)(2,1)}, u32[]{:S(2)}, u32[]{:S(2)}) async-start(bf16[2,256,256]{2,0,1:T(2,128)(2,1)} %copy.78), calls=%async_computation.7 | async-start | bytes 524288 | tf_op jit(solution)/shard_map/all_to_all | solution.py:100
  278.0 492.6 %all-reduce.9.cloned.1.call-start = ((), (), s32[]{:S(2)}) async-start(), calls=%async_computation.9 | async-start | bytes 786432 | tf_op jit(solution)/shard_map/psum | solution.py:88
Sparse Core Ops, SparseCore 0:
  305.3 465.2 all-reduce.8
where the time goes:
time: 781 us; the launch traced here: 779 us
  waiting for transfers between devices  598 us (77%)
  starting transfers between devices  73.9 us (9%)
  local copies, waits for them, and re-layouts  28.1 us (4%)
  blocking collectives  27.7 us (4%)
  other arithmetic  18.9 us (2%)
  matrix products  17.7 us (2%)
  between operations  14.5 us (2%)
    psum x1, waiting for transfers between devices, shards(): g_head_sum = lax.psum(g_head, ('crop', 'axial'))  465 us
    all_to_all x1, blocking collectives, shards(): lax.all_to_all(x_bar.astype(jnp.bfloat16), 'axial', split_axis=0, concat_...  27.7 us
    all_to_all x1, starting transfers between devices, shards(): lax.all_to_all(tb_bf, 'axial', split_axis=0, concat_axis=1, tiled=True)  21.3 us
    all_to_all x1, waiting for transfers between devices, shards(): lax.all_to_all(tb_bf, 'axial', split_axis=0, concat_axis=1, tiled=True)  20.7 us
    all_to_all x1, waiting for transfers between devices, shards(): lax.all_to_all(a_bf, 'axial', split_axis=0, concat_axis=1, tiled=True)  20 us
    all_to_all x1, waiting for transfers between devices, shards(): lax.all_to_all(ta_bf, 'axial', split_axis=0, concat_axis=1, tiled=True)  18.4 us
    all_to_all x1, waiting for transfers between devices, shards(): lax.all_to_all(b_bf, 'axial', split_axis=0, concat_axis=1, tiled=True)  16.7 us
    all_to_all x1, waiting for transfers between devices, shards(): lax.all_to_all(a_bar, 'axial', split_axis=1, concat_axis=0, tiled=True)  16.5 us
  transfers between devices with their start and end apart: 9, of which 9 were waited for; matrix products, arithmetic and copies ran while one was open for 3% of the time, Pallas kernels for 0%

commit v1 on v0

--- a/solution.py
+++ b/solution.py
@@ -85,7 +85,9 @@
     total = lax.axis_size("crop") * width * width
     cot = t_out * (1.0 / total)
     g_head, x_bar = pull_head(cot)
-    g_head_sum = lax.psum(g_head, ("crop", "axial"))
+    g_head_sum = g_head
+    for i0 in ("axial", "crop"):
+        g_head_sum = lax.psum(g_head_sum, axis_name=i0)
     xb_ch = lax.all_to_all(
         x_bar.astype(jnp.bfloat16), "axial", split_axis=0, concat_axis=1, tiled=True
     )

time: 781 us -> 1630 us (2.09)
  the two profiles are of different devices: /device:TPU:2 before, /device:TPU:4 now
where the time goes in v1:
time: 1630 us
  waiting for transfers between devices  1440 us (88%)
  starting transfers between devices  83.8 us (5%)
  local copies, waits for them, and re-layouts  28.1 us (2%)
  blocking collectives  28 us (2%)
  other arithmetic  18.9 us (1%)
  matrix products  17.6 us (1%)
    psum x2, waiting for transfers between devices, shards(): g_head_sum = lax.psum(g_head_sum, axis_name=i0)  856 us
    psum x1, waiting for transfers between devices, shards(): g_in_sum = lax.psum(g_in, ('crop', 'axial'))  471 us
  transfers between devices with their start and end apart: 11, of which 10 were waited for; matrix products, arithmetic and copies ran while one was open for 2% of the time, Pallas kernels for 0%

profile of v1, /device:TPU:4, one launch (start us, length us, event | category | flops | bytes accessed | tf_op | source)
XLA Modules:
  0.0 1628.2 jit_solution(13380235310690939671)
XLA Ops:
  13.0 1.8 fusion.63
  14.9 2.1 fusion.38
  18.0 21.3 %all-to-all-start.4 = ((bf16[128,4,256]{2,1,0:T(4,128)(2,1)}), bf16[128,4,256]{2,1,0:T(4,128)(2,1)S(1)}, u32[]{:S(2)}, u32[]{:S(2)}) async-start(bf16[128,4,256]{2,1,0:T(4,128)(2,1)} %copy.69), calls=%async_computation.4 | async-start | bytes 524288 | tf_op jit(solution)/shard_map/all_to_all | solution.py:73
  40.2 19.4 %all-to-all-done.4 = bf16[128,4,256]{2,1,0:T(4,128)(2,1)S(1)} async-done(((bf16[128,4,256]{2,1,0:T(4,128)(2,1)}), bf16[128,4,256]{2,1,0:T(4,128)(2,1)S(1)}, u32[]{:S(2)}, u32[]{:S(2)}) %all-to-all-start.4) | async-done | bytes 262176 | tf_op jit(solution)/shard_map/all_to_all | solution.py:73
  59.6 9.2 all-to-all-start.1
  69.6 15.2 all-to-all-done.1
  84.8 11.2 all-to-all-start
  96.9 18.5 %all-to-all-done = bf16[128,4,256]{2,1,0:T(4,128)(2,1)S(1)} async-done(((bf16[128,4,256]{2,1,0:T(4,128)(2,1)}), bf16[128,4,256]{2,1,0:T(4,128)(2,1)S(1)}, u32[]{:S(2)}, u32[]{:S(2)}) %all-to-all-start) | async-done | bytes 262176 | tf_op jit(solution)/shard_map/all_to_all | solution.py:68
  115.4 8.1 all-to-all-start.3
  126.1 16.9 %all-to-all-done.3 = bf16[128,4,256]{2,1,0:T(4,128)(2,1)} async-done(((bf16[128,4,256]{2,1,0:T(4,128)(2,1)}), bf16[128,4,256]{2,1,0:T(4,128)(2,1)}, u32[]{:S(2)}, u32[]{:S(2)}) %all-to-all-start.3) | async-done | bytes 262176 | tf_op jit(solution)/shard_map/all_to_all | solution.py:72
  143.1 7.5 all-to-all-start.2
  152.4 1.7 copy.66
  154.2 1.7 all_to_all.105
  158.4 12.2 all-to-all-done.2
  170.6 8.5 all-to-all-start.5
  184.8 13.8 all-to-all-done.5
  200.7 1.9 copy_bitcast_fusion
  202.6 2.2 reshape.106
  204.8 1.9 multiply_reduce_fusion
  212.8 28.0 %all_to_all.126 = bf16[128,4,256]{2,1,0:T(4,128)(2,1)S(1)} all-to-all(bf16[128,4,256]{2,1,0:T(4,128)(2,1)S(1)} %copy.75), channel_id=1, replica_groups=mesh['crop'=8,'axial'=64] {'axial'}, dimensions={0} | all-to-all | bytes 524288 | tf_op jit(solution)/shard_map/all_to_all | solution.py:91
  242.7 7.9 all-to-all-start.8
  252.9 15.1 all-to-all-done.8
  268.0 9.9 all-to-all-start.7
  281.7 771.4 %all-reduce.12.cloned.1.call-done = f32[128,256]{1,0:T(8,128)} async-done(((f32[128,256]{1,0:T(8,128)}), f32[128,256]{1,0:T(8,128)}) %all-reduce.12.cloned.1.call-update) | async-done | bytes 131088 | tf_op jit(solution)/shard_map/psum | solution.py:90
  1053.2 1.8 copy.83
  1055.0 2.0 copy.84
  1057.0 1.8 copy.79
  1058.9 2.1 copy.80
  1061.0 1.6 multiply_multiply_fusion.3
  1064.8 84.4 %all-reduce.14.cloned.1.call-done = f32[128,256]{1,0:T(8,128)} async-done(((f32[128,256]{1,0:T(8,128)}), f32[128,256]{1,0:T(8,128)}) %all-reduce.14.cloned.1.call-update) | async-done | bytes 131088 | tf_op jit(solution)/shard_map/psum | solution.py:90
  1149.2 470.7 %all-reduce.10.cloned.1.call-done = f32[128,512]{1,0:T(8,128)} async-done(((f32[128,512]{1,0:T(8,128)}), f32[128,512]{1,0:T(8,128)}) %all-reduce.10.cloned.1.call-update) | async-done | bytes 262160 | tf_op jit(solution)/shard_map/psum | solution.py:105
  1619.9 1.8 pad_maximum_fusion
  (91 shorter events, 40.2 us)
Async XLA Ops:
  7.2 5.8 copy-start
  11.4 3.4 copy-start.14
  18.0 41.6 %all-to-all-start.4 = ((bf16[128,4,256]{2,1,0:T(4,128)(2,1)}), bf16[128,4,256]{2,1,0:T(4,128)(2,1)S(1)}, u32[]{:S(2)}, u32[]{:S(2)}) async-start(bf16[128,4,256]{2,1,0:T(4,128)(2,1)} %copy.69), calls=%async_computation.4 | async-start | bytes 524288 | tf_op jit(solution)/shard_map/all_to_all | solution.py:73
  59.6 25.2 %all-to-all-start.1 = ((bf16[128,4,256]{2,1,0:T(4,128)(2,1)}), bf16[128,4,256]{2,1,0:T(4,128)(2,1)S(1)}, u32[]{:S(2)}, u32[]{:S(2)}) async-start(bf16[128,4,256]{2,1,0:T(4,128)(2,1)} %copy.57), calls=%async_computation.1 | async-start | bytes 524288 | tf_op jit(solution)/shard_map/all_to_all | solution.py:69
  84.8 30.6 %all-to-all-start = ((bf16[128,4,256]{2,1,0:T(4,128)(2,1)}), bf16[128,4,256]{2,1,0:T(4,128)(2,1)S(1)}, u32[]{:S(2)}, u32[]{:S(2)}) async-start(bf16[128,4,256]{2,1,0:T(4,128)(2,1)} %copy.55), calls=%async_computation | async-start | bytes 524288 | tf_op jit(solution)/shard_map/all_to_all | solution.py:68
  115.4 8.1 copy-start.13
  115.4 27.6 %all-to-all-start.3 = ((bf16[128,4,256]{2,1,0:T(4,128)(2,1)}), bf16[128,4,256]{2,1,0:T(4,128)(2,1)}, u32[]{:S(2)}, u32[]{:S(2)}) async-start(bf16[128,4,256]{2,1,0:T(4,128)(2,1)} %copy.65), calls=%async_computation.3 | async-start | bytes 524288 | tf_op jit(solution)/shard_map/all_to_all | solution.py:72
  123.7 32.2 %copy-start.8 = (bf16[2,256,256]{2,1,0:T(8,128)(2,1)}, bf16[2,256,256]{2,1,0:T(8,128)(2,1)S(1)}, u32[]{:S(2)}) copy-start(bf16[2,256,256]{2,1,0:T(8,128)(2,1)S(1)} %all_to_all.100) | copy-start | bytes 786436
  124.9 32.2 %copy-start.6 = (bf16[2,256,256]{2,1,0:T(8,128)(2,1)}, bf16[2,256,256]{2,1,0:T(8,128)(2,1)S(1)}, u32[]{:S(2)}) copy-start(bf16[2,256,256]{2,1,0:T(8,128)(2,1)S(1)} %all_to_all.96) | copy-start | bytes 786436
  143.1 27.5 %all-to-all-start.2 = ((bf16[2,256,256]{2,0,1:T(2,128)(2,1)}), bf16[2,256,256]{2,0,1:T(2,128)(2,1)S(1)}, u32[]{:S(2)}, u32[]{:S(2)}) async-start(bf16[2,256,256]{2,0,1:T(2,128)(2,1)} %copy.59), calls=%async_computation.2 | async-start | bytes 524288 | tf_op jit(solution)/shard_map/all_to_all | solution.py:77
  170.6 9.8 copy-start.10
  170.6 28.0 %all-to-all-start.5 = ((bf16[2,256,256]{2,0,1:T(2,128)(2,1)}), bf16[2,256,256]{2,0,1:T(2,128)(2,1)}, u32[]{:S(2)}, u32[]{:S(2)}) async-start(bf16[2,256,256]{2,0,1:T(2,128)(2,1)} %copy.71), calls=%async_computation.5 | async-start | bytes 524288 | tf_op jit(solution)/shard_map/all_to_all | solution.py:78
  183.9 0.8 copy-start.4
  199.7 0.8 copy-start.5
  204.8 3.0 copy-start.12
  206.8 2.2 copy-start.7
  207.8 3.4 copy-start.1
  211.2 1.4 copy-start.3
  212.3 28.7 %copy-start.9 = (bf16[2,256,256]{2,1,0:T(8,128)(2,1)S(1)}, bf16[2,256,256]{2,1,0:T(8,128)(2,1)}, u32[]{:S(2)}) copy-start(bf16[2,256,256]{2,1,0:T(8,128)(2,1)} %copy-done.8) | copy-start | bytes 786436
  241.0 0.7 copy-start.11
  241.7 37.7 %copy-start.2 = (f32[4,256,128]{2,1,0:T(8,128)S(1)}, f32[4,256,128]{2,1,0:T(8,128)}, u32[]{:S(2)}) copy-start(f32[4,256,128]{2,1,0:T(8,128)} %copy-done.1) | copy-start | bytes 1572868
  242.7 25.3 %all-to-all-start.8 = ((bf16[2,256,256]{2,0,1:T(2,128)(2,1)}), bf16[2,256,256]{2,0,1:T(2,128)(2,1)}, u32[]{:S(2)}, u32[]{:S(2)}) async-start(bf16[2,256,256]{2,0,1:T(2,128)(2,1)} %copy.82), calls=%async_computation.8 | async-start | bytes 524288 | tf_op jit(solution)/shard_map/all_to_all | solution.py:101
  268.0 789.0 %all-to-all-start.7 = ((bf16[2,256,256]{2,0,1:T(2,128)(2,1)}), bf16[2,256,256]{2,0,1:T(2,128)(2,1)}, u32[]{:S(2)}, u32[]{:S(2)}) async-start(bf16[2,256,256]{2,0,1:T(2,128)(2,1)} %copy.78), calls=%async_computation.7 | async-start | bytes 524288 | tf_op jit(solution)/shard_map/all_to_all | solution.py:102
  278.0 775.1 %all-reduce.12.cloned.1.call-start = ((), (), s32[]{:S(2)}) async-start(), calls=%async_computation.10 | async-start | bytes 262144 | tf_op jit(solution)/shard_map/psum | solution.py:90
  281.7 867.6 %all-reduce.14.cloned.1.call-start = ((), (), s32[]{:S(2)}) async-start(), calls=%async_computation.11 | async-start | bytes 262144 | tf_op jit(solution)/shard_map/psum | solution.py:90
  1053.1 566.8 %all-reduce.10.cloned.1.call-start = ((), (), s32[]{:S(2)}) async-start(), calls=%async_computation.9 | async-start | bytes 524288 | tf_op jit(solution)/shard_map/psum | solution.py:105
Sparse Core Ops, SparseCore 0:
  282.3 770.7 all-reduce.11
  1056.0 93.2 all-reduce.13
  1155.3 464.6 all-reduce.9
